TPU v7x, 256 devices: a whole 4x4x8 slice. The times are simulated.
256 devices in a mesh: row: 32 (over y, z), col: 8 (over x, core).
Axes of the slice: x: 4, y: 4, z: 8, core: 2. Of those that a mesh axis runs over, the one named last changes fastest.
Arguments:
- valence: bfloat16 [131072, 2048], P('row', 'col')
- conduction: bfloat16 [131072, 1024], P('row', 'col')
- point_index: int32 [8192], replicated, may hold values from 0 to 131071, as said below
Outputs:
- gram: float32 [8192, 8192], P('col', 'row')
Inputs may be any that keep to these rules, and one draw needn't show every extreme that they name: `point_index`: 8192 distinct cells; cell g lies in slab g // 4096. In each aligned block of 256 entries, at most 16 lie in any one slab, and in every block some slab holds exactly 16.
All inputs are finite; a program needn't handle non-finite values.
Results may differ from a plain program's by a relative error of at most 0.0003.
Values may be sent and summed in bfloat16 or wider, within the bound.
No kernel may reach another device: no remote copies, remote signals or barrier semaphores. Data moves between devices by JAX's collectives and lax.ppermute only.
A program may use at most 128 MiB of HBM per device.

v0:
```python
import functools

import jax
import jax.numpy as jnp
from jax import lax
from jax.experimental import pallas as pl
from jax.experimental.pallas import tpu as pltpu
from jax.sharding import Mesh, PartitionSpec as P


NY, NZ, NX, NK = 4, 8, 4, 2
AXES = ("y", "z", "x", "core")
CAP = 16
RING = (0, -1, 1, 2)


def route(where):
    pairs = []
    for y in range(NY):
        for z in range(NZ):
            for x in range(NX):
                for k in range(NK):
                    ty, tz, tx, tk = where(y, z, x, k)
                    src = ((y * NZ + z) * NX + x) * NK + k
                    dst = ((ty % NY * NZ + tz % NZ) * NX + tx % NX) * NK + tk % NK
                    pairs.append((src, dst))
    return pairs


def send(a, where):
    return lax.ppermute(a, AXES, route(where))


def first_ring(d):
    return lambda y, z, x, k: (y, z, x + d, k) if k == 0 else (y + d, z, x, k)


def second_ring(d):
    return lambda y, z, x, k: (y + d, z, x, k) if k == 0 else (y, z, x + d, k)


def z_ring(d):
    return lambda y, z, x, k: (y, z + d, x, k)


def y_ring(d):
    return lambda y, z, x, k: (y + d, z, x, k)


def other_core(y, z, x, k):
    return (y, z, x, 1 - k)


def held_block(y, z):
    return (y - z) & 3


def to_left_owner(y, z, x, k):
    block = held_block(y, z)
    return (block + z, z ^ (2 * x + k), block, z // 4)


def gather(piece):
    half = piece.shape[0] // 2
    left = [send(piece, to_left_owner)]
    across = send(piece, first_ring(2))
    minus, plus = send(piece, first_ring(1)), send(piece, first_ring(-1))
    mine = jnp.stack([piece, minus, plus, across])
    left += [send(left[0], z_ring(1)), send(left[0], z_ring(-1))]
    m, p = send(mine, second_ring(1)), send(mine, second_ring(-1))
    left += [send(left[1], z_ring(1)), send(left[2], z_ring(-1))]
    fm, fp = send(m[:2], second_ring(1)), send(p[2:], second_ring(-1))
    theirs = [send(jnp.concatenate([mine, m, p]), other_core)]
    left += [send(left[3], z_ring(1)), send(left[4], z_ring(-1))]
    theirs += [send(jnp.concatenate([fm, fp]), other_core)]
    left += [send(left[5][:half], z_ring(1)), send(left[6][half:], z_ring(-1))]
    return left, [mine, m, p, fm, fp], theirs


DIMS = (((1,), (1,)), ((), ()))


def contract(a, b):
    return lax.dot_general(a, b, DIMS, preferred_element_type=jnp.float32)


def columns(share, width):
    return pl.ds(pl.multiple_of(share * width, width), width)


def most_kernel(*refs):
    left, refs = refs[:7], refs[7:]
    (mine, theirs), refs = (refs[:5], refs[5:7]), refs[7:]
    (valence_sums, conduction_sums, last), (lv, lc, rv, rc) = refs[:3], refs[3:]
    y, z, x, k = (lax.axis_index(a) for a in AXES)
    rows = left[0].shape[0]
    nv = rv.shape[1] // (NX * NK)
    nc = rc.shape[1] // (NX * NK)
    zb = 4 * k + ((y - x) & 3)
    last_share = ((z + 4) & 7) ^ zb
    for ref, far in zip(left, (0, -1, 1, -2, 2, -3, 3)):
        share = ((z + far) & 7) ^ zb
        lv[:, columns(share, nv)] = ref[:, :nv]
        lc[:, columns(share, nc)] = ref[:, nv:]
    lv[:, columns(last_share, nv)] = jnp.zeros((rows, nv), lv.dtype)
    lc[:, columns(last_share, nc)] = jnp.zeros((rows, nc), lc.dtype)
    for i, a in enumerate(RING):
        for j, b in enumerate(RING):
            own = mine[i].at[j] if i < 3 else mine[3 + j // 2].at[j % 2]
            other = theirs[0].at[4 * i + j] if i < 3 else theirs[1].at[j]
            for ref, core in ((own, k), (other, 1 - k)):
                dy = jnp.where(core == 0, a, b)
                dx = jnp.where(core == 0, b, a)
                block = held_block(y + dy, z)
                share = 2 * ((x + dx) & 3) + core
                here = pl.ds(pl.multiple_of(block * rows, rows), rows)
                rv[here, columns(share, nv)] = ref[:, :nv]
                rc[here, columns(share, nc)] = ref[:, nv:]
    last[:, :nv] = rv[:, columns(last_share, nv)]
    last[:, nv:] = rc[:, columns(last_share, nc)]
    for a in range(NY):
        here = pl.ds(a * rows, rows)
        valence_sums[here, :] = contract(lv[...], rv[here, :])
        conduction_sums[here, :] = contract(lc[...], rc[here, :])


def rest_kernel(upper, lower, last, valence_sums, conduction_sums, *outs, nv):
    y = lax.axis_index("y")
    rows = outs[0].shape[0]
    half = rows // 2
    for e, out in enumerate(outs):
        here = pl.ds(pl.multiple_of(((e + y) & 3) * rows, rows), rows)
        right = last[here, :]
        gv, gc = valence_sums[here, :], conduction_sums[here, :]
        for at, ref in ((0, upper), (half, lower)):
            part = slice(at, at + half)
            out[part, :] = (gv[part] + contract(ref[:, :nv], right[:, :nv])) * (
                gc[part] + contract(ref[:, nv:], right[:, nv:])
            )


def gram_tiles(left, mine, theirs, nv):
    rows, width = left[0].shape
    nc = width - nv
    shares = NX * NK
    vmem = pl.BlockSpec(memory_space=pltpu.VMEM)
    sums = pl.pallas_call(
        most_kernel,
        out_shape=[jax.ShapeDtypeStruct((NY * rows, rows), jnp.float32)] * 2
        + [jax.ShapeDtypeStruct((NY * rows, width), jnp.bfloat16)],
        in_specs=[vmem] * 14,
        out_specs=[vmem] * 3,
        scratch_shapes=[
            pltpu.VMEM((rows, shares * nv), jnp.bfloat16),
            pltpu.VMEM((rows, shares * nc), jnp.bfloat16),
            pltpu.VMEM((NY * rows, shares * nv), jnp.bfloat16),
            pltpu.VMEM((NY * rows, shares * nc), jnp.bfloat16),
        ],
        compiler_params=pltpu.CompilerParams(vmem_limit_bytes=24 << 20),
        name="most",
    )(*left[:7], *mine, *theirs)
    return pl.pallas_call(
        functools.partial(rest_kernel, nv=nv),
        out_shape=[jax.ShapeDtypeStruct((rows, rows), jnp.float32)] * NY,
        in_specs=[vmem] * 5,
        out_specs=[vmem] * NY,
        compiler_params=pltpu.CompilerParams(vmem_limit_bytes=12 << 20),
        name="rest",
    )(*left[7:], sums[2], sums[0], sums[1])


def place_kernel(*refs):
    parts, out, sems = refs[:NY], refs[NY], refs[NY + 1]
    y, x = lax.axis_index("y"), lax.axis_index("x")
    rows = parts[0].shape[0]
    copies = []
    for e, ref in enumerate(parts):
        here = pl.ds(pl.multiple_of(((y + e - x) & 3) * rows, rows), rows)
        copies.append(pltpu.make_async_copy(ref, out.at[here, :], sems.at[e]))
        copies[-1].start()
    for copy in copies:
        copy.wait()


def place(parts):
    rows, width = parts[0].shape
    anywhere = pl.BlockSpec(memory_space=pl.ANY)
    return pl.pallas_call(
        place_kernel,
        out_shape=jax.ShapeDtypeStruct((NY * rows, width), jnp.float32),
        in_specs=[anywhere] * NY,
        out_specs=anywhere,
        scratch_shapes=[pltpu.SemaphoreType.DMA((NY,))],
        compiler_params=pltpu.CompilerParams(vmem_limit_bytes=1 << 20),
        name="place",
    )(*parts)


def pick_kernel(points, valence, conduction, outgoing, wanted, lift, val, cond, sems):
    copies = [
        pltpu.make_async_copy(valence, val, sems.at[0]),
        pltpu.make_async_copy(conduction, cond, sems.at[1]),
    ]
    for copy in copies:
        copy.start()
    n_row = NY * NZ
    cells = val.shape[0]
    width = val.shape[1]
    bits = cells.bit_length() - 1
    y, z = lax.axis_index("y"), lax.axis_index("z")
    lanes = points.shape[1]
    per_block = points.shape[0] // n_row * lanes

    def block_rows(first, count):
        parts = [points[pl.ds(first + i, count, stride=2), :] for i in range(2)]
        return jnp.concatenate(parts, axis=1)

    def iota(shape, dim):
        return lax.broadcasted_iota(jnp.int32, shape, dim)

    cell = block_rows(0, n_row)
    offset = (cell & (cells - 1)).astype(jnp.float32)
    owned = (cell >> bits) == y * NZ + z
    mine = 2 * (held_block(y, z) * NZ + z)
    own_owner = jnp.concatenate([points[pl.ds(mine + i, 1), :] for i in range(2)], axis=1) >> bits
    own_is = own_owner == iota((n_row, per_block), 0)
    earlier = iota((per_block, per_block), 0) < iota((per_block, per_block), 1)
    masks = jnp.concatenate([owned.astype(jnp.float32), own_is.astype(jnp.float32)])
    counts = jnp.dot(
        masks.astype(jnp.bfloat16),
        earlier.astype(jnp.float32).astype(jnp.bfloat16),
        preferred_element_type=jnp.float32,
    )
    rank = jnp.where(owned, counts[:n_row], -1.0)
    own_rank = jnp.sum(jnp.where(own_is, counts[n_row:], 0.0), axis=0, keepdims=True)
    own_slot = own_owner * CAP + own_rank.astype(jnp.int32)
    wanted[...] = (
        (iota((n_row * CAP, per_block), 0) == own_slot).astype(jnp.float32).astype(jnp.bfloat16)
    )
    slot = iota((CAP, per_block), 0).astype(jnp.float32)
    all_cells = iota((CAP, cells), 1)
    for d in range(n_row):
        b = held_block(d // NZ, d % NZ) * NZ + d % NZ
        here = rank[b : b + 1] == slot
        at = jnp.sum(jnp.where(here, offset[b : b + 1], 0.0), axis=1, keepdims=True)
        hot = (all_cells == at.astype(jnp.int32)).astype(jnp.float32)
        lift[pl.ds(d * CAP, CAP), :] = hot.astype(jnp.bfloat16)
    for copy in copies:
        copy.wait()
    for ref, columns_of in ((val, slice(0, width)), (cond, slice(width, None))):
        outgoing[:, columns_of] = jnp.dot(
            lift[...], ref[...], preferred_element_type=jnp.float32
        ).astype(jnp.bfloat16)


def pick(points, valence, conduction):
    vmem, anywhere = (pl.BlockSpec(memory_space=m) for m in (pltpu.VMEM, pl.ANY))
    n_row = NY * NZ
    width = valence.shape[1] + conduction.shape[1]
    return pl.pallas_call(
        pick_kernel,
        out_shape=[
            jax.ShapeDtypeStruct((n_row * CAP, width), jnp.bfloat16),
            jax.ShapeDtypeStruct((n_row * CAP, points.size // n_row), jnp.bfloat16),
        ],
        in_specs=[vmem, anywhere, anywhere],
        out_specs=[vmem] * 2,
        scratch_shapes=[
            pltpu.VMEM((n_row * CAP, valence.shape[0]), jnp.bfloat16),
            pltpu.VMEM(valence.shape, jnp.bfloat16),
            pltpu.VMEM(conduction.shape, jnp.bfloat16),
            pltpu.SemaphoreType.DMA((2,)),
        ],
        compiler_params=pltpu.CompilerParams(vmem_limit_bytes=20 << 20),
        name="pick",
    )(points, *(pltpu.with_memory_space_constraint(a, pltpu.HBM) for a in (valence, conduction)))


def compact_kernel(wanted, got, piece):
    piece[...] = lax.dot_general(
        wanted[...], got[...], (((0,), (0,)), ((), ())), preferred_element_type=jnp.float32
    ).astype(jnp.bfloat16)


def compact(wanted, got):
    vmem = pl.BlockSpec(memory_space=pltpu.VMEM)
    return pl.pallas_call(
        compact_kernel,
        out_shape=jax.ShapeDtypeStruct((wanted.shape[1], got.shape[1]), jnp.bfloat16),
        in_specs=[vmem] * 2,
        out_specs=vmem,
        compiler_params=pltpu.CompilerParams(vmem_limit_bytes=4 << 20),
        name="compact",
    )(wanted, got)


def tiles_of(valence, conduction, point_index):
    n_row = NY * NZ
    outgoing, wanted = pick(point_index.reshape(-1, 128), valence, conduction)
    got = lax.all_to_all(
        outgoing.reshape(n_row, CAP, -1), ("y", "z"), split_axis=0, concat_axis=0, tiled=True
    )
    piece = compact(wanted, got.reshape(n_row * CAP, -1))

    left, mine, theirs = gather(piece)
    tiles = gram_tiles(left, mine, theirs, valence.shape[1])
    parts = [tiles[0]]
    for e in range(1, NY):
        parts.append(send(tiles[(-e) % NY], y_ring(-e)))
    return place(parts)


def solution(mesh):
    fine = Mesh(mesh.devices.reshape(NY, NZ, NX, NK), AXES)
    row, col = ("y", "z"), ("x", "core")
    return jax.shard_map(
        tiles_of,
        mesh=fine,
        in_specs=(P(row, col), P(row, col), P()),
        out_specs=P(col, row),
        check_vma=False,
    )
```

profile of v0, /device:TPU:1, one launch (start us, length us, event | category | flops | bytes accessed | tf_op | source)
XLA Modules:
  0.0 122.4 jit_solution(13646401089874374410)
XLA Ops:
  0.8 5.3 %pick.1 = (bf16[512,384]{1,0:T(8,128)(2,1)S(1)}, bf16[512,256]{1,0:T(8,128)(2,1)S(1)}) custom-call(s32[64,128]{1,0:T(8,128)S(1)} %bitcast.14, bf16[4096,256]{1,0:T(8,128)(2,1)} %valence.1, bf16[4096,128]{1,0:T(8,128)(2,1)} %conduction.1), custom_call_target="tpu_custom_call" | custom-call | tf_op jit(solution)/shard_map/pick/pallas_call | solution.py:260
  6.1 23.5 %all_to_all.5 = bf16[32,16,384]{2,1,0:T(8,128)(2,1)S(1)} all-to-all(bf16[32,16,384]{2,1,0:T(8,128)(2,1)S(1)} %bitcast.13), channel_id=1, replica_groups=mesh['y'=4,'z'=8,'x'=4,'core'=2] {'y','z'}, dimensions={0} | all-to-all | bytes 786432 | tf_op jit(solution)/shard_map/all_to_all | solution.py:300
  30.6 2.1 %collective-permute-start.10 = (bf16[256,384]{1,0:T(8,128)(2,1)S(1)}, bf16[256,384]{1,0:T(8,128)(2,1)S(1)}, u32[]{:S(2)}, u32[]{:S(2)}) collective-permute-start(bf16[256,384]{1,0:T(8,128)(2,1)S(1)} %compact.1), channel_id=1, source_target_pairs={{0,6},{1,193},{2,0},{3,195},{4,2},{5,197},{6,4},{7,199},{8,14},{9,... | collective-permute-start | bytes 589832 | tf_op jit(solution)/shard_map/ppermute | solution.py:31
  33.3 2.4 %collective-permute-done.9 = bf16[256,384]{1,0:T(8,128)(2,1)S(1)} collective-permute-done((bf16[256,384]{1,0:T(8,128)(2,1)S(1)}, bf16[256,384]{1,0:T(8,128)(2,1)S(1)}, u32[]{:S(2)}, u32[]{:S(2)}) %collective-permute-start.9) | collective-permute-done | bytes 196640 | tf_op jit(solution)/shard_map/ppermute | solution.py:31
  35.7 1.7 %collective-permute-done.10 = bf16[256,384]{1,0:T(8,128)(2,1)S(1)} collective-permute-done((bf16[256,384]{1,0:T(8,128)(2,1)S(1)}, bf16[256,384]{1,0:T(8,128)(2,1)S(1)}, u32[]{:S(2)}, u32[]{:S(2)}) %collective-permute-start.10) | collective-permute-done | bytes 196640 | tf_op jit(solution)/shard_map/ppermute | solution.py:31
  37.4 1.3 %collective-permute-done.11 = bf16[256,384]{1,0:T(8,128)(2,1)S(1)} collective-permute-done((bf16[256,384]{1,0:T(8,128)(2,1)S(1)}, bf16[256,384]{1,0:T(8,128)(2,1)S(1)}, u32[]{:S(2)}, u32[]{:S(2)}) %collective-permute-start.11) | collective-permute-done | bytes 196640 | tf_op jit(solution)/shard_map/ppermute | solution.py:31
  40.2 1.5 %collective-permute-start.13 = (bf16[4,256,384]{2,1,0:T(8,128)(2,1)S(1)}, bf16[4,256,384]{2,1,0:T(8,128)(2,1)S(1)}, u32[]{:S(2)}, u32[]{:S(2)}) collective-permute-start(bf16[4,256,384]{2,1,0:T(8,128)(2,1)S(1)} %pad_maximum_fusion.refs_7_), channel_id=1, source_target_pairs={{0,192},{1,7},{2,194},{3,1},{4,196},{5,3},{6,198},{7,5},{8,200},{9... | collective-permute-start | bytes 2359304 | tf_op jit(solution)/shard_map/ppermute | solution.py:31
  41.8 10.3 %collective-permute-done.12.refs_8_ = bf16[4,256,384]{2,1,0:T(8,128)(2,1)S(1)} collective-permute-done((bf16[4,256,384]{2,1,0:T(8,128)(2,1)S(1)}, bf16[4,256,384]{2,1,0:T(8,128)(2,1)S(1)}, u32[]{:S(2)}, u32[]{:S(2)}) %collective-permute-start.12) | collective-permute-done | bytes 786464 | tf_op jit(solution)/shard_map/ppermute | solution.py:31
  52.5 5.6 %collective-permute-start.16 = (bf16[12,256,384]{2,1,0:T(8,128)(2,1)S(1)}, bf16[12,256,384]{2,1,0:T(8,128)(2,1)S(1)}, u32[]{:S(2)}, u32[]{:S(2)}) collective-permute-start(bf16[12,256,384]{2,1,0:T(8,128)(2,1)S(1)} %constant_dynamic-update-slice_fusion), channel_id=1, source_target_pairs={{0,1},{1,0},{2,3},{3,2},{4,5},{5,4},{6,7},{7,6},{8,9},{9,8},{10,11... | collective-permute-start | bytes 7077896 | tf_op jit(solution)/shard_map/ppermute | solution.py:31
  58.8 2.1 %collective-permute-start.15 = (bf16[2,256,384]{2,1,0:T(8,128)(2,1)S(1)}, bf16[2,256,384]{2,1,0:T(8,128)(2,1)S(1)}, u32[]{:S(2)}, u32[]{:S(2)}) collective-permute-start(bf16[2,256,384]{2,1,0:T(8,128)(2,1)S(1)} %slice.19), channel_id=1, source_target_pairs={{0,192},{1,7},{2,194},{3,1},{4,196},{5,3},{6,198},{7,5},{8,200},{9... | collective-permute-start | bytes 1179656 | tf_op jit(solution)/shard_map/ppermute | solution.py:31
  60.9 4.2 %collective-permute-start = (bf16[256,384]{1,0:T(8,128)(2,1)S(1)}, bf16[256,384]{1,0:T(8,128)(2,1)S(1)}, u32[]{:S(2)}, u32[]{:S(2)}) collective-permute-start(bf16[256,384]{1,0:T(8,128)(2,1)S(1)} %compact.1), channel_id=1, source_target_pairs={{0,0},{1,8},{2,16},{3,24},{4,32},{5,40},{6,48},{7,56},{8,14},{9,6}... | collective-permute-start | bytes 589832 | tf_op jit(solution)/shard_map/ppermute | solution.py:31
  67.4 7.7 %collective-permute-done.refs_0_ = bf16[256,384]{1,0:T(8,128)(2,1)S(1)} collective-permute-done((bf16[256,384]{1,0:T(8,128)(2,1)S(1)}, bf16[256,384]{1,0:T(8,128)(2,1)S(1)}, u32[]{:S(2)}, u32[]{:S(2)}) %collective-permute-start) | collective-permute-done | bytes 196640 | tf_op jit(solution)/shard_map/ppermute | solution.py:31
  75.0 4.1 %collective-permute-start.1 = (bf16[256,384]{1,0:T(8,128)(2,1)S(1)}, bf16[256,384]{1,0:T(8,128)(2,1)S(1)}, u32[]{:S(2)}, u32[]{:S(2)}) collective-permute-start(bf16[256,384]{1,0:T(8,128)(2,1)S(1)} %collective-permute-done.refs_0_), channel_id=1, source_target_pairs={{0,8},{1,9},{2,10},{3,11},{4,12},{5,13},{6,14},{7,15},{8,16},{9,17... | collective-permute-start | bytes 589832 | tf_op jit(solution)/shard_map/ppermute | solution.py:31
  79.1 3.6 %collective-permute-done.1.refs_1_ = bf16[256,384]{1,0:T(8,128)(2,1)S(1)} collective-permute-done((bf16[256,384]{1,0:T(8,128)(2,1)S(1)}, bf16[256,384]{1,0:T(8,128)(2,1)S(1)}, u32[]{:S(2)}, u32[]{:S(2)}) %collective-permute-start.1) | collective-permute-done | bytes 196640 | tf_op jit(solution)/shard_map/ppermute | solution.py:31
  83.6 2.6 %collective-permute-start.6 = (bf16[256,384]{1,0:T(8,128)(2,1)S(1)}, bf16[256,384]{1,0:T(8,128)(2,1)S(1)}, u32[]{:S(2)}, u32[]{:S(2)}) collective-permute-start(bf16[256,384]{1,0:T(8,128)(2,1)S(1)} %collective-permute-done.5.refs_2_), channel_id=1, source_target_pairs={{0,56},{1,57},{2,58},{3,59},{4,60},{5,61},{6,62},{7,63},{8,0},{9,1... | collective-permute-start | bytes 589832 | tf_op jit(solution)/shard_map/ppermute | solution.py:31
  86.3 3.3 %collective-permute-done.2.refs_3_ = bf16[256,384]{1,0:T(8,128)(2,1)S(1)} collective-permute-done((bf16[256,384]{1,0:T(8,128)(2,1)S(1)}, bf16[256,384]{1,0:T(8,128)(2,1)S(1)}, u32[]{:S(2)}, u32[]{:S(2)}) %collective-permute-start.2) | collective-permute-done | bytes 196640 | tf_op jit(solution)/shard_map/ppermute | solution.py:31
  90.4 3.3 %collective-permute-start.7 = (bf16[256,384]{1,0:T(8,128)(2,1)S(1)}, bf16[256,384]{1,0:T(8,128)(2,1)S(1)}, u32[]{:S(2)}, u32[]{:S(2)}) collective-permute-start(bf16[256,384]{1,0:T(8,128)(2,1)S(1)} %collective-permute-done.6.refs_4_), channel_id=1, source_target_pairs={{0,56},{1,57},{2,58},{3,59},{4,60},{5,61},{6,62},{7,63},{8,0},{9,1... | collective-permute-start | bytes 589832 | tf_op jit(solution)/shard_map/ppermute | solution.py:31
  93.7 1.6 %collective-permute-done.3.refs_5_ = bf16[256,384]{1,0:T(8,128)(2,1)S(1)} collective-permute-done((bf16[256,384]{1,0:T(8,128)(2,1)S(1)}, bf16[256,384]{1,0:T(8,128)(2,1)S(1)}, u32[]{:S(2)}, u32[]{:S(2)}) %collective-permute-start.3) | collective-permute-done | bytes 196640 | tf_op jit(solution)/shard_map/ppermute | solution.py:31
  96.8 3.5 %collective-permute-start.8 = (bf16[128,384]{1,0:T(8,128)(2,1)S(1)}, bf16[128,384]{1,0:T(8,128)(2,1)S(1)}, u32[]{:S(2)}, u32[]{:S(2)}) collective-permute-start(bf16[128,384]{1,0:T(8,128)(2,1)S(1)} %slice.17), channel_id=1, source_target_pairs={{0,56},{1,57},{2,58},{3,59},{4,60},{5,61},{6,62},{7,63},{8,0},{9,1... | collective-permute-start | bytes 294920 | tf_op jit(solution)/shard_map/ppermute | solution.py:31
  100.3 3.3 %most.1 = (f32[1024,256]{1,0:T(8,128)S(1)}, f32[1024,256]{1,0:T(8,128)S(1)}, bf16[1024,384]{1,0:T(8,128)(2,1)S(1)}) custom-call(bf16[256,384]{1,0:T(8,128)(2,1)S(1)} %collective-permute-done.refs_0_, bf16[256,384]{1,0:T(8,128)(2,1)S(1)} %collective-permute-done.1.refs_1_, bf16[256,384]{1,0:T(8,128)(2,1)S(1)} %collective-permute-done.5.refs_2_, ...), custom_call_target="tpu_custom_call" | custom-call | tf_op jit(solution)/shard_map/most/pallas_call | solution.py:147
  104.2 2.6 %collective-permute-start.18 = (f32[256,256]{1,0:T(8,128)S(1)}, f32[256,256]{1,0:T(8,128)S(1)}, u32[]{:S(2)}, u32[]{:S(2)}) collective-permute-start(f32[256,256]{1,0:T(8,128)S(1)} %get-tuple-element.20), channel_id=1, source_target_pairs={{0,192},{1,193},{2,194},{3,195},{4,196},{5,197},{6,198},{7,199},{8... | collective-permute-start | bytes 786440 | tf_op jit(solution)/shard_map/ppermute | solution.py:31
  107.5 5.1 %collective-permute-done.18.refs_1_ = f32[256,256]{1,0:T(8,128)S(1)} collective-permute-done((f32[256,256]{1,0:T(8,128)S(1)}, f32[256,256]{1,0:T(8,128)S(1)}, u32[]{:S(2)}, u32[]{:S(2)}) %collective-permute-start.18) | collective-permute-done | bytes 262176 | tf_op jit(solution)/shard_map/ppermute | solution.py:31
  112.6 1.6 %collective-permute-done.19.refs_2_ = f32[256,256]{1,0:T(8,128)S(1)} collective-permute-done((f32[256,256]{1,0:T(8,128)S(1)}, f32[256,256]{1,0:T(8,128)S(1)}, u32[]{:S(2)}, u32[]{:S(2)}) %collective-permute-start.19) | collective-permute-done | bytes 262176 | tf_op jit(solution)/shard_map/ppermute | solution.py:31
  114.2 7.0 %collective-permute-done.20.refs_3_ = f32[256,256]{1,0:T(8,128)S(1)} collective-permute-done((f32[256,256]{1,0:T(8,128)S(1)}, f32[256,256]{1,0:T(8,128)S(1)}, u32[]{:S(2)}, u32[]{:S(2)}) %collective-permute-start.20) | collective-permute-done | bytes 262176 | tf_op jit(solution)/shard_map/ppermute | solution.py:31
  (38 shorter events, 12.7 us)
Async XLA Ops:
  0.0 0.8 copy-start
  29.9 5.8 %collective-permute-start.9 = (bf16[256,384]{1,0:T(8,128)(2,1)S(1)}, bf16[256,384]{1,0:T(8,128)(2,1)S(1)}, u32[]{:S(2)}, u32[]{:S(2)}) collective-permute-start(bf16[256,384]{1,0:T(8,128)(2,1)S(1)} %compact.1), channel_id=1, source_target_pairs={{0,2},{1,65},{2,4},{3,67},{4,6},{5,69},{6,0},{7,71},{8,10},{9,73},... | collective-permute-start | bytes 589832 | tf_op jit(solution)/shard_map/ppermute | solution.py:31
  30.6 6.8 %collective-permute-start.10 = (bf16[256,384]{1,0:T(8,128)(2,1)S(1)}, bf16[256,384]{1,0:T(8,128)(2,1)S(1)}, u32[]{:S(2)}, u32[]{:S(2)}) collective-permute-start(bf16[256,384]{1,0:T(8,128)(2,1)S(1)} %compact.1), channel_id=1, source_target_pairs={{0,6},{1,193},{2,0},{3,195},{4,2},{5,197},{6,4},{7,199},{8,14},{9,... | collective-permute-start | bytes 589832 | tf_op jit(solution)/shard_map/ppermute | solution.py:31
  32.7 6.0 %collective-permute-start.11 = (bf16[256,384]{1,0:T(8,128)(2,1)S(1)}, bf16[256,384]{1,0:T(8,128)(2,1)S(1)}, u32[]{:S(2)}, u32[]{:S(2)}) collective-permute-start(bf16[256,384]{1,0:T(8,128)(2,1)S(1)} %compact.1), channel_id=1, source_target_pairs={{0,4},{1,129},{2,6},{3,131},{4,0},{5,133},{6,2},{7,135},{8,12},{9,... | collective-permute-start | bytes 589832 | tf_op jit(solution)/shard_map/ppermute | solution.py:31
  38.8 13.3 %collective-permute-start.12 = (bf16[4,256,384]{2,1,0:T(8,128)(2,1)S(1)}, bf16[4,256,384]{2,1,0:T(8,128)(2,1)S(1)}, u32[]{:S(2)}, u32[]{:S(2)}) collective-permute-start(bf16[4,256,384]{2,1,0:T(8,128)(2,1)S(1)} %pad_maximum_fusion.refs_7_), channel_id=1, source_target_pairs={{0,64},{1,3},{2,66},{3,5},{4,68},{5,7},{6,70},{7,1},{8,72},{9,11},... | collective-permute-start | bytes 2359304 | tf_op jit(solution)/shard_map/ppermute | solution.py:31
  40.2 12.1 %collective-permute-start.13 = (bf16[4,256,384]{2,1,0:T(8,128)(2,1)S(1)}, bf16[4,256,384]{2,1,0:T(8,128)(2,1)S(1)}, u32[]{:S(2)}, u32[]{:S(2)}) collective-permute-start(bf16[4,256,384]{2,1,0:T(8,128)(2,1)S(1)} %pad_maximum_fusion.refs_7_), channel_id=1, source_target_pairs={{0,192},{1,7},{2,194},{3,1},{4,196},{5,3},{6,198},{7,5},{8,200},{9... | collective-permute-start | bytes 2359304 | tf_op jit(solution)/shard_map/ppermute | solution.py:31
  52.5 47.9 %collective-permute-start.16 = (bf16[12,256,384]{2,1,0:T(8,128)(2,1)S(1)}, bf16[12,256,384]{2,1,0:T(8,128)(2,1)S(1)}, u32[]{:S(2)}, u32[]{:S(2)}) collective-permute-start(bf16[12,256,384]{2,1,0:T(8,128)(2,1)S(1)} %constant_dynamic-update-slice_fusion), channel_id=1, source_target_pairs={{0,1},{1,0},{2,3},{3,2},{4,5},{5,4},{6,7},{7,6},{8,9},{9,8},{10,11... | collective-permute-start | bytes 7077896 | tf_op jit(solution)/shard_map/ppermute | solution.py:31
  58.1 8.2 %collective-permute-start.14 = (bf16[2,256,384]{2,1,0:T(8,128)(2,1)S(1)}, bf16[2,256,384]{2,1,0:T(8,128)(2,1)S(1)}, u32[]{:S(2)}, u32[]{:S(2)}) collective-permute-start(bf16[2,256,384]{2,1,0:T(8,128)(2,1)S(1)} %slice.18), channel_id=1, source_target_pairs={{0,64},{1,3},{2,66},{3,5},{4,68},{5,7},{6,70},{7,1},{8,72},{9,11},... | collective-permute-start | bytes 1179656 | tf_op jit(solution)/shard_map/ppermute | solution.py:31
  58.8 7.5 %collective-permute-start.15 = (bf16[2,256,384]{2,1,0:T(8,128)(2,1)S(1)}, bf16[2,256,384]{2,1,0:T(8,128)(2,1)S(1)}, u32[]{:S(2)}, u32[]{:S(2)}) collective-permute-start(bf16[2,256,384]{2,1,0:T(8,128)(2,1)S(1)} %slice.19), channel_id=1, source_target_pairs={{0,192},{1,7},{2,194},{3,1},{4,196},{5,3},{6,198},{7,5},{8,200},{9... | collective-permute-start | bytes 1179656 | tf_op jit(solution)/shard_map/ppermute | solution.py:31
  60.9 14.1 %collective-permute-start = (bf16[256,384]{1,0:T(8,128)(2,1)S(1)}, bf16[256,384]{1,0:T(8,128)(2,1)S(1)}, u32[]{:S(2)}, u32[]{:S(2)}) collective-permute-start(bf16[256,384]{1,0:T(8,128)(2,1)S(1)} %compact.1), channel_id=1, source_target_pairs={{0,0},{1,8},{2,16},{3,24},{4,32},{5,40},{6,48},{7,56},{8,14},{9,6}... | collective-permute-start | bytes 589832 | tf_op jit(solution)/shard_map/ppermute | solution.py:31
  66.4 34.0 %collective-permute-start.17 = (bf16[4,256,384]{2,1,0:T(8,128)(2,1)S(1)}, bf16[4,256,384]{2,1,0:T(8,128)(2,1)S(1)}, u32[]{:S(2)}, u32[]{:S(2)}) collective-permute-start(bf16[4,256,384]{2,1,0:T(8,128)(2,1)S(1)} %pad_maximum_fusion.1), channel_id=1, source_target_pairs={{0,1},{1,0},{2,3},{3,2},{4,5},{5,4},{6,7},{7,6},{8,9},{9,8},{10,11... | collective-permute-start | bytes 2359304 | tf_op jit(solution)/shard_map/ppermute | solution.py:31
  75.0 7.7 %collective-permute-start.1 = (bf16[256,384]{1,0:T(8,128)(2,1)S(1)}, bf16[256,384]{1,0:T(8,128)(2,1)S(1)}, u32[]{:S(2)}, u32[]{:S(2)}) collective-permute-start(bf16[256,384]{1,0:T(8,128)(2,1)S(1)} %collective-permute-done.refs_0_), channel_id=1, source_target_pairs={{0,8},{1,9},{2,10},{3,11},{4,12},{5,13},{6,14},{7,15},{8,16},{9,17... | collective-permute-start | bytes 589832 | tf_op jit(solution)/shard_map/ppermute | solution.py:31
  79.1 4.5 %collective-permute-start.5 = (bf16[256,384]{1,0:T(8,128)(2,1)S(1)}, bf16[256,384]{1,0:T(8,128)(2,1)S(1)}, u32[]{:S(2)}, u32[]{:S(2)}) collective-permute-start(bf16[256,384]{1,0:T(8,128)(2,1)S(1)} %collective-permute-done.refs_0_), channel_id=1, source_target_pairs={{0,56},{1,57},{2,58},{3,59},{4,60},{5,61},{6,62},{7,63},{8,0},{9,1... | collective-permute-start | bytes 589832 | tf_op jit(solution)/shard_map/ppermute | solution.py:31
  82.7 6.8 %collective-permute-start.2 = (bf16[256,384]{1,0:T(8,128)(2,1)S(1)}, bf16[256,384]{1,0:T(8,128)(2,1)S(1)}, u32[]{:S(2)}, u32[]{:S(2)}) collective-permute-start(bf16[256,384]{1,0:T(8,128)(2,1)S(1)} %collective-permute-done.1.refs_1_), channel_id=1, source_target_pairs={{0,8},{1,9},{2,10},{3,11},{4,12},{5,13},{6,14},{7,15},{8,16},{9,17... | collective-permute-start | bytes 589832 | tf_op jit(solution)/shard_map/ppermute | solution.py:31
  83.6 6.8 %collective-permute-start.6 = (bf16[256,384]{1,0:T(8,128)(2,1)S(1)}, bf16[256,384]{1,0:T(8,128)(2,1)S(1)}, u32[]{:S(2)}, u32[]{:S(2)}) collective-permute-start(bf16[256,384]{1,0:T(8,128)(2,1)S(1)} %collective-permute-done.5.refs_2_), channel_id=1, source_target_pairs={{0,56},{1,57},{2,58},{3,59},{4,60},{5,61},{6,62},{7,63},{8,0},{9,1... | collective-permute-start | bytes 589832 | tf_op jit(solution)/shard_map/ppermute | solution.py:31
  89.6 5.7 %collective-permute-start.3 = (bf16[256,384]{1,0:T(8,128)(2,1)S(1)}, bf16[256,384]{1,0:T(8,128)(2,1)S(1)}, u32[]{:S(2)}, u32[]{:S(2)}) collective-permute-start(bf16[256,384]{1,0:T(8,128)(2,1)S(1)} %collective-permute-done.2.refs_3_), channel_id=1, source_target_pairs={{0,8},{1,9},{2,10},{3,11},{4,12},{5,13},{6,14},{7,15},{8,16},{9,17... | collective-permute-start | bytes 589832 | tf_op jit(solution)/shard_map/ppermute | solution.py:31
  90.4 6.4 %collective-permute-start.7 = (bf16[256,384]{1,0:T(8,128)(2,1)S(1)}, bf16[256,384]{1,0:T(8,128)(2,1)S(1)}, u32[]{:S(2)}, u32[]{:S(2)}) collective-permute-start(bf16[256,384]{1,0:T(8,128)(2,1)S(1)} %collective-permute-done.6.refs_4_), channel_id=1, source_target_pairs={{0,56},{1,57},{2,58},{3,59},{4,60},{5,61},{6,62},{7,63},{8,0},{9,1... | collective-permute-start | bytes 589832 | tf_op jit(solution)/shard_map/ppermute | solution.py:31
  95.3 8.3 %collective-permute-start.4 = (bf16[128,384]{1,0:T(8,128)(2,1)S(1)}, bf16[128,384]{1,0:T(8,128)(2,1)S(1)}, u32[]{:S(2)}, u32[]{:S(2)}) collective-permute-start(bf16[128,384]{1,0:T(8,128)(2,1)S(1)} %slice.16), channel_id=1, source_target_pairs={{0,8},{1,9},{2,10},{3,11},{4,12},{5,13},{6,14},{7,15},{8,16},{9,17... | collective-permute-start | bytes 294920 | tf_op jit(solution)/shard_map/ppermute | solution.py:31
  96.8 6.8 %collective-permute-start.8 = (bf16[128,384]{1,0:T(8,128)(2,1)S(1)}, bf16[128,384]{1,0:T(8,128)(2,1)S(1)}, u32[]{:S(2)}, u32[]{:S(2)}) collective-permute-start(bf16[128,384]{1,0:T(8,128)(2,1)S(1)} %slice.17), channel_id=1, source_target_pairs={{0,56},{1,57},{2,58},{3,59},{4,60},{5,61},{6,62},{7,63},{8,0},{9,1... | collective-permute-start | bytes 294920 | tf_op jit(solution)/shard_map/ppermute | solution.py:31
  104.2 8.4 %collective-permute-start.18 = (f32[256,256]{1,0:T(8,128)S(1)}, f32[256,256]{1,0:T(8,128)S(1)}, u32[]{:S(2)}, u32[]{:S(2)}) collective-permute-start(f32[256,256]{1,0:T(8,128)S(1)} %get-tuple-element.20), channel_id=1, source_target_pairs={{0,192},{1,193},{2,194},{3,195},{4,196},{5,197},{6,198},{7,199},{8... | collective-permute-start | bytes 786440 | tf_op jit(solution)/shard_map/ppermute | solution.py:31
  106.8 7.4 %collective-permute-start.19 = (f32[256,256]{1,0:T(8,128)S(1)}, f32[256,256]{1,0:T(8,128)S(1)}, u32[]{:S(2)}, u32[]{:S(2)}) collective-permute-start(f32[256,256]{1,0:T(8,128)S(1)} %get-tuple-element.21), channel_id=1, source_target_pairs={{0,128},{1,129},{2,130},{3,131},{4,132},{5,133},{6,134},{7,135},{8... | collective-permute-start | bytes 786440 | tf_op jit(solution)/shard_map/ppermute | solution.py:31
  106.8 14.4 %collective-permute-start.20 = (f32[256,256]{1,0:T(8,128)S(1)}, f32[256,256]{1,0:T(8,128)S(1)}, u32[]{:S(2)}, u32[]{:S(2)}) collective-permute-start(f32[256,256]{1,0:T(8,128)S(1)} %get-tuple-element.22), channel_id=1, source_target_pairs={{0,64},{1,65},{2,66},{3,67},{4,68},{5,69},{6,70},{7,71},{8,72},{9,... | collective-permute-start | bytes 786440 | tf_op jit(solution)/shard_map/ppermute | solution.py:31
where the time goes:
time: 123 us; the launch traced here: 122 us
  waiting for transfers between devices  47.2 us (38%)
  starting transfers between devices  39.3 us (32%)
  blocking collectives  23.5 us (19%)
  Pallas kernels  10.5 us (9%)
  local copies, waits for them, and re-layouts  1.27 us (1%)
    ppermute x21, waiting for transfers between devices, send(): return lax.ppermute(a, AXES, route(where))  47.2 us
    ppermute x21, starting transfers between devices, send(): return lax.ppermute(a, AXES, route(where))  39.3 us
    all_to_all x1, blocking collectives, tiles_of(): lax.all_to_all(outgoing.reshape(n_row, CAP, -1), ('y', 'z'), split_axis=0...  23.5 us
    pallas_call x1, Pallas kernels, pick(): pl.pallas_call(pick_kernel, out_shape=[jax.ShapeDtypeStruct((n_row * CAP,...  5.3 us
    pallas_call x1, Pallas kernels, gram_tiles(): pl.pallas_call(most_kernel, out_shape=[jax.ShapeDtypeStruct((NY * rows, r...  3.31 us
  transfers between devices with their start and end apart: 21, of which 13 were waited for; matrix products, arithmetic and copies ran while one was open for 0% of the time, Pallas kernels for 3%

commit v1 on v0

--- a/solution.py
+++ b/solution.py
@@ -239,18 +239,22 @@
     )
     slot = iota((CAP, per_block), 0).astype(jnp.float32)
     all_cells = iota((CAP, cells), 1)
-    for d in range(n_row):
-        b = held_block(d // NZ, d % NZ) * NZ + d % NZ
-        here = rank[b : b + 1] == slot
-        at = jnp.sum(jnp.where(here, offset[b : b + 1], 0.0), axis=1, keepdims=True)
-        hot = (all_cells == at.astype(jnp.int32)).astype(jnp.float32)
-        lift[pl.ds(d * CAP, CAP), :] = hot.astype(jnp.bfloat16)
-    for copy in copies:
-        copy.wait()
-    for ref, columns_of in ((val, slice(0, width)), (cond, slice(width, None))):
-        outgoing[:, columns_of] = jnp.dot(
-            lift[...], ref[...], preferred_element_type=jnp.float32
-        ).astype(jnp.bfloat16)
+    per_group = n_row // 4
+    for first in range(0, n_row, per_group):
+        for d in range(first, first + per_group):
+            b = held_block(d // NZ, d % NZ) * NZ + d % NZ
+            here = rank[b : b + 1] == slot
+            at = jnp.sum(jnp.where(here, offset[b : b + 1], 0.0), axis=1, keepdims=True)
+            hot = (all_cells == at.astype(jnp.int32)).astype(jnp.float32)
+            lift[pl.ds(d * CAP, CAP), :] = hot.astype(jnp.bfloat16)
+        if first == 0:
+            for copy in copies:
+                copy.wait()
+        rows = pl.ds(first * CAP, per_group * CAP)
+        for ref, columns_of in ((val, slice(0, width)), (cond, slice(width, None))):
+            outgoing[rows, columns_of] = jnp.dot(
+                lift[rows, :], ref[...], preferred_element_type=jnp.float32
+            ).astype(jnp.bfloat16)
 
 
 def pick(points, valence, conduction):

time: 123 us -> 122 us (level)
  no operation moved by 1% of the time
where the time goes in v1:
time: 122 us
  waiting for transfers between devices  47.2 us (39%)
  starting transfers between devices  39.4 us (32%)
  blocking collectives  23.5 us (19%)
  Pallas kernels  9.73 us (8%)
  local copies, waits for them, and re-layouts  1.27 us (1%)
    ppermute x21, waiting for transfers between devices, send(): return lax.ppermute(a, AXES, route(where))  47.2 us
    ppermute x21, starting transfers between devices, send(): return lax.ppermute(a, AXES, route(where))  39.4 us
    all_to_all x1, blocking collectives, tiles_of(): lax.all_to_all(outgoing.reshape(n_row, CAP, -1), ('y', 'z'), split_axis=0...  23.5 us
    pallas_call x1, Pallas kernels, pick(): pl.pallas_call(pick_kernel, out_shape=[jax.ShapeDtypeStruct((n_row * CAP,...  4.53 us
    pallas_call x1, Pallas kernels, gram_tiles(): pl.pallas_call(most_kernel, out_shape=[jax.ShapeDtypeStruct((NY * rows, r...  3.31 us
  transfers between devices with their start and end apart: 21, of which 13 were waited for; matrix products, arithmetic and copies ran while one was open for 0% of the time, Pallas kernels for 3%

profile of v1, /device:TPU:1, one launch (start us, length us, event | category | flops | bytes accessed | tf_op | source)
XLA Modules:
  0.0 121.6 jit_solution(12165149627501814958)
XLA Ops:
  0.8 4.5 %pick.1 = (bf16[512,384]{1,0:T(8,128)(2,1)S(1)}, bf16[512,256]{1,0:T(8,128)(2,1)S(1)}) custom-call(s32[64,128]{1,0:T(8,128)S(1)} %bitcast.14, bf16[4096,256]{1,0:T(8,128)(2,1)} %valence.1, bf16[4096,128]{1,0:T(8,128)(2,1)} %conduction.1), custom_call_target="tpu_custom_call" | custom-call | tf_op jit(solution)/shard_map/pick/pallas_call | solution.py:264
  5.3 23.5 %all_to_all.5 = bf16[32,16,384]{2,1,0:T(8,128)(2,1)S(1)} all-to-all(bf16[32,16,384]{2,1,0:T(8,128)(2,1)S(1)} %bitcast.13), channel_id=1, replica_groups=mesh['y'=4,'z'=8,'x'=4,'core'=2] {'y','z'}, dimensions={0} | all-to-all | bytes 786432 | tf_op jit(solution)/shard_map/all_to_all | solution.py:304
  29.8 2.1 %collective-permute-start.10 = (bf16[256,384]{1,0:T(8,128)(2,1)S(1)}, bf16[256,384]{1,0:T(8,128)(2,1)S(1)}, u32[]{:S(2)}, u32[]{:S(2)}) collective-permute-start(bf16[256,384]{1,0:T(8,128)(2,1)S(1)} %compact.1), channel_id=1, source_target_pairs={{0,6},{1,193},{2,0},{3,195},{4,2},{5,197},{6,4},{7,199},{8,14},{9,... | collective-permute-start | bytes 589832 | tf_op jit(solution)/shard_map/ppermute | solution.py:31
  32.5 2.4 %collective-permute-done.9 = bf16[256,384]{1,0:T(8,128)(2,1)S(1)} collective-permute-done((bf16[256,384]{1,0:T(8,128)(2,1)S(1)}, bf16[256,384]{1,0:T(8,128)(2,1)S(1)}, u32[]{:S(2)}, u32[]{:S(2)}) %collective-permute-start.9) | collective-permute-done | bytes 196640 | tf_op jit(solution)/shard_map/ppermute | solution.py:31
  35.0 1.7 %collective-permute-done.10 = bf16[256,384]{1,0:T(8,128)(2,1)S(1)} collective-permute-done((bf16[256,384]{1,0:T(8,128)(2,1)S(1)}, bf16[256,384]{1,0:T(8,128)(2,1)S(1)}, u32[]{:S(2)}, u32[]{:S(2)}) %collective-permute-start.10) | collective-permute-done | bytes 196640 | tf_op jit(solution)/shard_map/ppermute | solution.py:31
  36.6 1.3 %collective-permute-done.11 = bf16[256,384]{1,0:T(8,128)(2,1)S(1)} collective-permute-done((bf16[256,384]{1,0:T(8,128)(2,1)S(1)}, bf16[256,384]{1,0:T(8,128)(2,1)S(1)}, u32[]{:S(2)}, u32[]{:S(2)}) %collective-permute-start.11) | collective-permute-done | bytes 196640 | tf_op jit(solution)/shard_map/ppermute | solution.py:31
  39.4 1.5 %collective-permute-start.13 = (bf16[4,256,384]{2,1,0:T(8,128)(2,1)S(1)}, bf16[4,256,384]{2,1,0:T(8,128)(2,1)S(1)}, u32[]{:S(2)}, u32[]{:S(2)}) collective-permute-start(bf16[4,256,384]{2,1,0:T(8,128)(2,1)S(1)} %pad_maximum_fusion.refs_7_), channel_id=1, source_target_pairs={{0,192},{1,7},{2,194},{3,1},{4,196},{5,3},{6,198},{7,5},{8,200},{9... | collective-permute-start | bytes 2359304 | tf_op jit(solution)/shard_map/ppermute | solution.py:31
  41.0 10.3 %collective-permute-done.12.refs_8_ = bf16[4,256,384]{2,1,0:T(8,128)(2,1)S(1)} collective-permute-done((bf16[4,256,384]{2,1,0:T(8,128)(2,1)S(1)}, bf16[4,256,384]{2,1,0:T(8,128)(2,1)S(1)}, u32[]{:S(2)}, u32[]{:S(2)}) %collective-permute-start.12) | collective-permute-done | bytes 786464 | tf_op jit(solution)/shard_map/ppermute | solution.py:31
  51.7 5.6 %collective-permute-start.16 = (bf16[12,256,384]{2,1,0:T(8,128)(2,1)S(1)}, bf16[12,256,384]{2,1,0:T(8,128)(2,1)S(1)}, u32[]{:S(2)}, u32[]{:S(2)}) collective-permute-start(bf16[12,256,384]{2,1,0:T(8,128)(2,1)S(1)} %constant_dynamic-update-slice_fusion), channel_id=1, source_target_pairs={{0,1},{1,0},{2,3},{3,2},{4,5},{5,4},{6,7},{7,6},{8,9},{9,8},{10,11... | collective-permute-start | bytes 7077896 | tf_op jit(solution)/shard_map/ppermute | solution.py:31
  58.0 2.1 %collective-permute-start.15 = (bf16[2,256,384]{2,1,0:T(8,128)(2,1)S(1)}, bf16[2,256,384]{2,1,0:T(8,128)(2,1)S(1)}, u32[]{:S(2)}, u32[]{:S(2)}) collective-permute-start(bf16[2,256,384]{2,1,0:T(8,128)(2,1)S(1)} %slice.19), channel_id=1, source_target_pairs={{0,192},{1,7},{2,194},{3,1},{4,196},{5,3},{6,198},{7,5},{8,200},{9... | collective-permute-start | bytes 1179656 | tf_op jit(solution)/shard_map/ppermute | solution.py:31
  60.2 4.2 %collective-permute-start = (bf16[256,384]{1,0:T(8,128)(2,1)S(1)}, bf16[256,384]{1,0:T(8,128)(2,1)S(1)}, u32[]{:S(2)}, u32[]{:S(2)}) collective-permute-start(bf16[256,384]{1,0:T(8,128)(2,1)S(1)} %compact.1), channel_id=1, source_target_pairs={{0,0},{1,8},{2,16},{3,24},{4,32},{5,40},{6,48},{7,56},{8,14},{9,6}... | collective-permute-start | bytes 589832 | tf_op jit(solution)/shard_map/ppermute | solution.py:31
  66.6 7.7 %collective-permute-done.refs_0_ = bf16[256,384]{1,0:T(8,128)(2,1)S(1)} collective-permute-done((bf16[256,384]{1,0:T(8,128)(2,1)S(1)}, bf16[256,384]{1,0:T(8,128)(2,1)S(1)}, u32[]{:S(2)}, u32[]{:S(2)}) %collective-permute-start) | collective-permute-done | bytes 196640 | tf_op jit(solution)/shard_map/ppermute | solution.py:31
  74.2 4.1 %collective-permute-start.1 = (bf16[256,384]{1,0:T(8,128)(2,1)S(1)}, bf16[256,384]{1,0:T(8,128)(2,1)S(1)}, u32[]{:S(2)}, u32[]{:S(2)}) collective-permute-start(bf16[256,384]{1,0:T(8,128)(2,1)S(1)} %collective-permute-done.refs_0_), channel_id=1, source_target_pairs={{0,8},{1,9},{2,10},{3,11},{4,12},{5,13},{6,14},{7,15},{8,16},{9,17... | collective-permute-start | bytes 589832 | tf_op jit(solution)/shard_map/ppermute | solution.py:31
  78.3 3.6 %collective-permute-done.1.refs_1_ = bf16[256,384]{1,0:T(8,128)(2,1)S(1)} collective-permute-done((bf16[256,384]{1,0:T(8,128)(2,1)S(1)}, bf16[256,384]{1,0:T(8,128)(2,1)S(1)}, u32[]{:S(2)}, u32[]{:S(2)}) %collective-permute-start.1) | collective-permute-done | bytes 196640 | tf_op jit(solution)/shard_map/ppermute | solution.py:31
  82.8 2.6 %collective-permute-start.6 = (bf16[256,384]{1,0:T(8,128)(2,1)S(1)}, bf16[256,384]{1,0:T(8,128)(2,1)S(1)}, u32[]{:S(2)}, u32[]{:S(2)}) collective-permute-start(bf16[256,384]{1,0:T(8,128)(2,1)S(1)} %collective-permute-done.5.refs_2_), channel_id=1, source_target_pairs={{0,56},{1,57},{2,58},{3,59},{4,60},{5,61},{6,62},{7,63},{8,0},{9,1... | collective-permute-start | bytes 589832 | tf_op jit(solution)/shard_map/ppermute | solution.py:31
  85.5 3.3 %collective-permute-done.2.refs_3_ = bf16[256,384]{1,0:T(8,128)(2,1)S(1)} collective-permute-done((bf16[256,384]{1,0:T(8,128)(2,1)S(1)}, bf16[256,384]{1,0:T(8,128)(2,1)S(1)}, u32[]{:S(2)}, u32[]{:S(2)}) %collective-permute-start.2) | collective-permute-done | bytes 196640 | tf_op jit(solution)/shard_map/ppermute | solution.py:31
  89.6 3.3 %collective-permute-start.7 = (bf16[256,384]{1,0:T(8,128)(2,1)S(1)}, bf16[256,384]{1,0:T(8,128)(2,1)S(1)}, u32[]{:S(2)}, u32[]{:S(2)}) collective-permute-start(bf16[256,384]{1,0:T(8,128)(2,1)S(1)} %collective-permute-done.6.refs_4_), channel_id=1, source_target_pairs={{0,56},{1,57},{2,58},{3,59},{4,60},{5,61},{6,62},{7,63},{8,0},{9,1... | collective-permute-start | bytes 589832 | tf_op jit(solution)/shard_map/ppermute | solution.py:31
  92.9 1.6 %collective-permute-done.3.refs_5_ = bf16[256,384]{1,0:T(8,128)(2,1)S(1)} collective-permute-done((bf16[256,384]{1,0:T(8,128)(2,1)S(1)}, bf16[256,384]{1,0:T(8,128)(2,1)S(1)}, u32[]{:S(2)}, u32[]{:S(2)}) %collective-permute-start.3) | collective-permute-done | bytes 196640 | tf_op jit(solution)/shard_map/ppermute | solution.py:31
  96.1 3.5 %collective-permute-start.8 = (bf16[128,384]{1,0:T(8,128)(2,1)S(1)}, bf16[128,384]{1,0:T(8,128)(2,1)S(1)}, u32[]{:S(2)}, u32[]{:S(2)}) collective-permute-start(bf16[128,384]{1,0:T(8,128)(2,1)S(1)} %slice.17), channel_id=1, source_target_pairs={{0,56},{1,57},{2,58},{3,59},{4,60},{5,61},{6,62},{7,63},{8,0},{9,1... | collective-permute-start | bytes 294920 | tf_op jit(solution)/shard_map/ppermute | solution.py:31
  99.6 3.3 %most.1 = (f32[1024,256]{1,0:T(8,128)S(1)}, f32[1024,256]{1,0:T(8,128)S(1)}, bf16[1024,384]{1,0:T(8,128)(2,1)S(1)}) custom-call(bf16[256,384]{1,0:T(8,128)(2,1)S(1)} %collective-permute-done.refs_0_, bf16[256,384]{1,0:T(8,128)(2,1)S(1)} %collective-permute-done.1.refs_1_, bf16[256,384]{1,0:T(8,128)(2,1)S(1)} %collective-permute-done.5.refs_2_, ...), custom_call_target="tpu_custom_call" | custom-call | tf_op jit(solution)/shard_map/most/pallas_call | solution.py:147
  103.5 2.6 %collective-permute-start.18 = (f32[256,256]{1,0:T(8,128)S(1)}, f32[256,256]{1,0:T(8,128)S(1)}, u32[]{:S(2)}, u32[]{:S(2)}) collective-permute-start(f32[256,256]{1,0:T(8,128)S(1)} %get-tuple-element.20), channel_id=1, source_target_pairs={{0,192},{1,193},{2,194},{3,195},{4,196},{5,197},{6,198},{7,199},{8... | collective-permute-start | bytes 786440 | tf_op jit(solution)/shard_map/ppermute | solution.py:31
  106.7 5.1 %collective-permute-done.18.refs_1_ = f32[256,256]{1,0:T(8,128)S(1)} collective-permute-done((f32[256,256]{1,0:T(8,128)S(1)}, f32[256,256]{1,0:T(8,128)S(1)}, u32[]{:S(2)}, u32[]{:S(2)}) %collective-permute-start.18) | collective-permute-done | bytes 262176 | tf_op jit(solution)/shard_map/ppermute | solution.py:31
  111.8 1.6 %collective-permute-done.19.refs_2_ = f32[256,256]{1,0:T(8,128)S(1)} collective-permute-done((f32[256,256]{1,0:T(8,128)S(1)}, f32[256,256]{1,0:T(8,128)S(1)}, u32[]{:S(2)}, u32[]{:S(2)}) %collective-permute-start.19) | collective-permute-done | bytes 262176 | tf_op jit(solution)/shard_map/ppermute | solution.py:31
  113.4 7.0 %collective-permute-done.20.refs_3_ = f32[256,256]{1,0:T(8,128)S(1)} collective-permute-done((f32[256,256]{1,0:T(8,128)S(1)}, f32[256,256]{1,0:T(8,128)S(1)}, u32[]{:S(2)}, u32[]{:S(2)}) %collective-permute-start.20) | collective-permute-done | bytes 262176 | tf_op jit(solution)/shard_map/ppermute | solution.py:31
  (38 shorter events, 12.8 us)
Async XLA Ops:
  0.0 0.8 copy-start
  29.2 5.8 %collective-permute-start.9 = (bf16[256,384]{1,0:T(8,128)(2,1)S(1)}, bf16[256,384]{1,0:T(8,128)(2,1)S(1)}, u32[]{:S(2)}, u32[]{:S(2)}) collective-permute-start(bf16[256,384]{1,0:T(8,128)(2,1)S(1)} %compact.1), channel_id=1, source_target_pairs={{0,2},{1,65},{2,4},{3,67},{4,6},{5,69},{6,0},{7,71},{8,10},{9,73},... | collective-permute-start | bytes 589832 | tf_op jit(solution)/shard_map/ppermute | solution.py:31
  29.8 6.8 %collective-permute-start.10 = (bf16[256,384]{1,0:T(8,128)(2,1)S(1)}, bf16[256,384]{1,0:T(8,128)(2,1)S(1)}, u32[]{:S(2)}, u32[]{:S(2)}) collective-permute-start(bf16[256,384]{1,0:T(8,128)(2,1)S(1)} %compact.1), channel_id=1, source_target_pairs={{0,6},{1,193},{2,0},{3,195},{4,2},{5,197},{6,4},{7,199},{8,14},{9,... | collective-permute-start | bytes 589832 | tf_op jit(solution)/shard_map/ppermute | solution.py:31
  31.9 6.0 %collective-permute-start.11 = (bf16[256,384]{1,0:T(8,128)(2,1)S(1)}, bf16[256,384]{1,0:T(8,128)(2,1)S(1)}, u32[]{:S(2)}, u32[]{:S(2)}) collective-permute-start(bf16[256,384]{1,0:T(8,128)(2,1)S(1)} %compact.1), channel_id=1, source_target_pairs={{0,4},{1,129},{2,6},{3,131},{4,0},{5,133},{6,2},{7,135},{8,12},{9,... | collective-permute-start | bytes 589832 | tf_op jit(solution)/shard_map/ppermute | solution.py:31
  38.1 13.3 %collective-permute-start.12 = (bf16[4,256,384]{2,1,0:T(8,128)(2,1)S(1)}, bf16[4,256,384]{2,1,0:T(8,128)(2,1)S(1)}, u32[]{:S(2)}, u32[]{:S(2)}) collective-permute-start(bf16[4,256,384]{2,1,0:T(8,128)(2,1)S(1)} %pad_maximum_fusion.refs_7_), channel_id=1, source_target_pairs={{0,64},{1,3},{2,66},{3,5},{4,68},{5,7},{6,70},{7,1},{8,72},{9,11},... | collective-permute-start | bytes 2359304 | tf_op jit(solution)/shard_map/ppermute | solution.py:31
  39.4 12.1 %collective-permute-start.13 = (bf16[4,256,384]{2,1,0:T(8,128)(2,1)S(1)}, bf16[4,256,384]{2,1,0:T(8,128)(2,1)S(1)}, u32[]{:S(2)}, u32[]{:S(2)}) collective-permute-start(bf16[4,256,384]{2,1,0:T(8,128)(2,1)S(1)} %pad_maximum_fusion.refs_7_), channel_id=1, source_target_pairs={{0,192},{1,7},{2,194},{3,1},{4,196},{5,3},{6,198},{7,5},{8,200},{9... | collective-permute-start | bytes 2359304 | tf_op jit(solution)/shard_map/ppermute | solution.py:31
  51.7 47.9 %collective-permute-start.16 = (bf16[12,256,384]{2,1,0:T(8,128)(2,1)S(1)}, bf16[12,256,384]{2,1,0:T(8,128)(2,1)S(1)}, u32[]{:S(2)}, u32[]{:S(2)}) collective-permute-start(bf16[12,256,384]{2,1,0:T(8,128)(2,1)S(1)} %constant_dynamic-update-slice_fusion), channel_id=1, source_target_pairs={{0,1},{1,0},{2,3},{3,2},{4,5},{5,4},{6,7},{7,6},{8,9},{9,8},{10,11... | collective-permute-start | bytes 7077896 | tf_op jit(solution)/shard_map/ppermute | solution.py:31
  57.3 8.2 %collective-permute-start.14 = (bf16[2,256,384]{2,1,0:T(8,128)(2,1)S(1)}, bf16[2,256,384]{2,1,0:T(8,128)(2,1)S(1)}, u32[]{:S(2)}, u32[]{:S(2)}) collective-permute-start(bf16[2,256,384]{2,1,0:T(8,128)(2,1)S(1)} %slice.18), channel_id=1, source_target_pairs={{0,64},{1,3},{2,66},{3,5},{4,68},{5,7},{6,70},{7,1},{8,72},{9,11},... | collective-permute-start | bytes 1179656 | tf_op jit(solution)/shard_map/ppermute | solution.py:31
  58.0 7.5 %collective-permute-start.15 = (bf16[2,256,384]{2,1,0:T(8,128)(2,1)S(1)}, bf16[2,256,384]{2,1,0:T(8,128)(2,1)S(1)}, u32[]{:S(2)}, u32[]{:S(2)}) collective-permute-start(bf16[2,256,384]{2,1,0:T(8,128)(2,1)S(1)} %slice.19), channel_id=1, source_target_pairs={{0,192},{1,7},{2,194},{3,1},{4,196},{5,3},{6,198},{7,5},{8,200},{9... | collective-permute-start | bytes 1179656 | tf_op jit(solution)/shard_map/ppermute | solution.py:31
  60.2 14.1 %collective-permute-start = (bf16[256,384]{1,0:T(8,128)(2,1)S(1)}, bf16[256,384]{1,0:T(8,128)(2,1)S(1)}, u32[]{:S(2)}, u32[]{:S(2)}) collective-permute-start(bf16[256,384]{1,0:T(8,128)(2,1)S(1)} %compact.1), channel_id=1, source_target_pairs={{0,0},{1,8},{2,16},{3,24},{4,32},{5,40},{6,48},{7,56},{8,14},{9,6}... | collective-permute-start | bytes 589832 | tf_op jit(solution)/shard_map/ppermute | solution.py:31
  65.6 34.0 %collective-permute-start.17 = (bf16[4,256,384]{2,1,0:T(8,128)(2,1)S(1)}, bf16[4,256,384]{2,1,0:T(8,128)(2,1)S(1)}, u32[]{:S(2)}, u32[]{:S(2)}) collective-permute-start(bf16[4,256,384]{2,1,0:T(8,128)(2,1)S(1)} %pad_maximum_fusion.1), channel_id=1, source_target_pairs={{0,1},{1,0},{2,3},{3,2},{4,5},{5,4},{6,7},{7,6},{8,9},{9,8},{10,11... | collective-permute-start | bytes 2359304 | tf_op jit(solution)/shard_map/ppermute | solution.py:31
  74.2 7.7 %collective-permute-start.1 = (bf16[256,384]{1,0:T(8,128)(2,1)S(1)}, bf16[256,384]{1,0:T(8,128)(2,1)S(1)}, u32[]{:S(2)}, u32[]{:S(2)}) collective-permute-start(bf16[256,384]{1,0:T(8,128)(2,1)S(1)} %collective-permute-done.refs_0_), channel_id=1, source_target_pairs={{0,8},{1,9},{2,10},{3,11},{4,12},{5,13},{6,14},{7,15},{8,16},{9,17... | collective-permute-start | bytes 589832 | tf_op jit(solution)/shard_map/ppermute | solution.py:31
  78.3 4.5 %collective-permute-start.5 = (bf16[256,384]{1,0:T(8,128)(2,1)S(1)}, bf16[256,384]{1,0:T(8,128)(2,1)S(1)}, u32[]{:S(2)}, u32[]{:S(2)}) collective-permute-start(bf16[256,384]{1,0:T(8,128)(2,1)S(1)} %collective-permute-done.refs_0_), channel_id=1, source_target_pairs={{0,56},{1,57},{2,58},{3,59},{4,60},{5,61},{6,62},{7,63},{8,0},{9,1... | collective-permute-start | bytes 589832 | tf_op jit(solution)/shard_map/ppermute | solution.py:31
  81.9 6.8 %collective-permute-start.2 = (bf16[256,384]{1,0:T(8,128)(2,1)S(1)}, bf16[256,384]{1,0:T(8,128)(2,1)S(1)}, u32[]{:S(2)}, u32[]{:S(2)}) collective-permute-start(bf16[256,384]{1,0:T(8,128)(2,1)S(1)} %collective-permute-done.1.refs_1_), channel_id=1, source_target_pairs={{0,8},{1,9},{2,10},{3,11},{4,12},{5,13},{6,14},{7,15},{8,16},{9,17... | collective-permute-start | bytes 589832 | tf_op jit(solution)/shard_map/ppermute | solution.py:31
  82.8 6.8 %collective-permute-start.6 = (bf16[256,384]{1,0:T(8,128)(2,1)S(1)}, bf16[256,384]{1,0:T(8,128)(2,1)S(1)}, u32[]{:S(2)}, u32[]{:S(2)}) collective-permute-start(bf16[256,384]{1,0:T(8,128)(2,1)S(1)} %collective-permute-done.5.refs_2_), channel_id=1, source_target_pairs={{0,56},{1,57},{2,58},{3,59},{4,60},{5,61},{6,62},{7,63},{8,0},{9,1... | collective-permute-start | bytes 589832 | tf_op jit(solution)/shard_map/ppermute | solution.py:31
  88.8 5.7 %collective-permute-start.3 = (bf16[256,384]{1,0:T(8,128)(2,1)S(1)}, bf16[256,384]{1,0:T(8,128)(2,1)S(1)}, u32[]{:S(2)}, u32[]{:S(2)}) collective-permute-start(bf16[256,384]{1,0:T(8,128)(2,1)S(1)} %collective-permute-done.2.refs_3_), channel_id=1, source_target_pairs={{0,8},{1,9},{2,10},{3,11},{4,12},{5,13},{6,14},{7,15},{8,16},{9,17... | collective-permute-start | bytes 589832 | tf_op jit(solution)/shard_map/ppermute | solution.py:31
  89.6 6.4 %collective-permute-start.7 = (bf16[256,384]{1,0:T(8,128)(2,1)S(1)}, bf16[256,384]{1,0:T(8,128)(2,1)S(1)}, u32[]{:S(2)}, u32[]{:S(2)}) collective-permute-start(bf16[256,384]{1,0:T(8,128)(2,1)S(1)} %collective-permute-done.6.refs_4_), channel_id=1, source_target_pairs={{0,56},{1,57},{2,58},{3,59},{4,60},{5,61},{6,62},{7,63},{8,0},{9,1... | collective-permute-start | bytes 589832 | tf_op jit(solution)/shard_map/ppermute | solution.py:31
  94.5 8.4 %collective-permute-start.4 = (bf16[128,384]{1,0:T(8,128)(2,1)S(1)}, bf16[128,384]{1,0:T(8,128)(2,1)S(1)}, u32[]{:S(2)}, u32[]{:S(2)}) collective-permute-start(bf16[128,384]{1,0:T(8,128)(2,1)S(1)} %slice.16), channel_id=1, source_target_pairs={{0,8},{1,9},{2,10},{3,11},{4,12},{5,13},{6,14},{7,15},{8,16},{9,17... | collective-permute-start | bytes 294920 | tf_op jit(solution)/shard_map/ppermute | solution.py:31
  96.1 6.8 %collective-permute-start.8 = (bf16[128,384]{1,0:T(8,128)(2,1)S(1)}, bf16[128,384]{1,0:T(8,128)(2,1)S(1)}, u32[]{:S(2)}, u32[]{:S(2)}) collective-permute-start(bf16[128,384]{1,0:T(8,128)(2,1)S(1)} %slice.17), channel_id=1, source_target_pairs={{0,56},{1,57},{2,58},{3,59},{4,60},{5,61},{6,62},{7,63},{8,0},{9,1... | collective-permute-start | bytes 294920 | tf_op jit(solution)/shard_map/ppermute | solution.py:31
  103.5 8.4 %collective-permute-start.18 = (f32[256,256]{1,0:T(8,128)S(1)}, f32[256,256]{1,0:T(8,128)S(1)}, u32[]{:S(2)}, u32[]{:S(2)}) collective-permute-start(f32[256,256]{1,0:T(8,128)S(1)} %get-tuple-element.20), channel_id=1, source_target_pairs={{0,192},{1,193},{2,194},{3,195},{4,196},{5,197},{6,198},{7,199},{8... | collective-permute-start | bytes 786440 | tf_op jit(solution)/shard_map/ppermute | solution.py:31
  106.1 7.4 %collective-permute-start.19 = (f32[256,256]{1,0:T(8,128)S(1)}, f32[256,256]{1,0:T(8,128)S(1)}, u32[]{:S(2)}, u32[]{:S(2)}) collective-permute-start(f32[256,256]{1,0:T(8,128)S(1)} %get-tuple-element.21), channel_id=1, source_target_pairs={{0,128},{1,129},{2,130},{3,131},{4,132},{5,133},{6,134},{7,135},{8... | collective-permute-start | bytes 786440 | tf_op jit(solution)/shard_map/ppermute | solution.py:31
  106.1 14.4 %collective-permute-start.20 = (f32[256,256]{1,0:T(8,128)S(1)}, f32[256,256]{1,0:T(8,128)S(1)}, u32[]{:S(2)}, u32[]{:S(2)}) collective-permute-start(f32[256,256]{1,0:T(8,128)S(1)} %get-tuple-element.22), channel_id=1, source_target_pairs={{0,64},{1,65},{2,66},{3,67},{4,68},{5,69},{6,70},{7,71},{8,72},{9,... | collective-permute-start | bytes 786440 | tf_op jit(solution)/shard_map/ppermute | solution.py:31
